TPU v7x, 8 devices: a whole 2x2x1 slice. The times are simulated.
8 devices in a mesh: dp: 1 (over z), ep: 8 (over y, x, core).
Axes of the slice: x: 2, y: 2, z: 1, core: 2. Of those that a mesh axis runs over, the one named last changes fastest.
Arguments:
- tokens: bfloat16 [4096, 1280], P(('dp', 'ep'))
- expert_ids: int32 [4096, 6], P(('dp', 'ep'))
- gate_vals: float32 [4096, 6], P(('dp', 'ep'))
- slots: int32 [4096, 6], P(('dp', 'ep'))
- shared_w1: bfloat16 [1280, 1792], replicated
- shared_w3: bfloat16 [1280, 1792], replicated
- shared_w2: bfloat16 [1792, 1280], replicated
- shared_gate: bfloat16 [1280], replicated
- expert_w1: bfloat16 [64, 1280, 896], P('ep')
- expert_w3: bfloat16 [64, 1280, 896], P('ep')
- expert_w2: bfloat16 [64, 896, 1280], P('ep')
Outputs:
- output: bfloat16 [4096, 1280], P(('dp', 'ep'))
All inputs are finite; a program needn't handle non-finite values.
Results may differ from a plain program's by a relative error of at most 0.00517131.
Values are sent between devices in bfloat16 or wider.
A program may use at most 1 GiB of HBM per device.

v0:
```python
import jax
import jax.numpy as jnp
from jax import lax
from jax.sharding import PartitionSpec as P


def solution(mesh):
    num_ep = mesh.shape['ep']
    row_spec = P(('dp', 'ep'), None)
    replicated = P()
    expert_spec = P('ep', None, None)

    def device_step(tokens, expert_ids, gate_vals, slots, shared_w1, shared_w3, shared_w2, shared_gate, expert_w1, expert_w3, expert_w2):
        tok_count, hidden = tokens.shape
        top_k = expert_ids.shape[1]
        local_experts = expert_w1.shape[0]
        num_experts = local_experts * num_ep
        capacity = 8 * ((2 * tok_count * top_k + 8 * num_experts - 1) // (8 * num_experts))
        buf_rows = num_experts * capacity
        kept_mask = slots >= 0
        slot_dest = jnp.where(kept_mask, expert_ids * capacity + slots, buf_rows)
        copy_tok = jnp.arange(tok_count * top_k, dtype=jnp.int32) // top_k
        row_owner = jnp.full((buf_rows + 1,), tok_count, jnp.int32).at[slot_dest.reshape(-1)].set(copy_tok)
        send_buf = jnp.take(tokens, row_owner[:buf_rows], axis=0, mode='fill', fill_value=0)
        recv_buf = lax.all_to_all(send_buf.reshape(num_ep, local_experts * capacity, hidden), 'ep', 0, 0, tiled=True)
        expert_in = recv_buf.reshape(num_ep, local_experts, capacity, hidden)
        act_a = jnp.einsum('secd,edf->secf', expert_in, expert_w1, preferred_element_type=jnp.float32)
        act_b = jnp.einsum('secd,edf->secf', expert_in, expert_w3, preferred_element_type=jnp.float32)
        hidden_act = (jax.nn.silu(act_a) * act_b).astype(jnp.bfloat16)
        expert_out = jnp.einsum('secf,efd->secd', hidden_act, expert_w2, preferred_element_type=jnp.float32).astype(jnp.bfloat16)
        back_buf = lax.all_to_all(expert_out.reshape(num_ep, local_experts * capacity, hidden), 'ep', 0, 0, tiled=True)
        picked = jnp.take(back_buf.reshape(buf_rows, hidden), slot_dest, axis=0, mode='fill', fill_value=0)
        weights = jnp.where(kept_mask, gate_vals, 0.0)[:, :, None]
        routed = jnp.sum(weights * picked, axis=1)
        gate_logit = jnp.dot(tokens, shared_gate, preferred_element_type=jnp.float32)
        shared_a = jnp.dot(tokens, shared_w1, preferred_element_type=jnp.float32)
        shared_b = jnp.dot(tokens, shared_w3, preferred_element_type=jnp.float32)
        shared_h = (jax.nn.silu(shared_a) * shared_b).astype(jnp.bfloat16)
        shared_out = jnp.dot(shared_h, shared_w2, preferred_element_type=jnp.float32)
        total = tokens.astype(jnp.float32) + jax.nn.sigmoid(gate_logit)[:, None] * shared_out + routed
        return total.astype(jnp.bfloat16)

    return jax.shard_map(device_step, mesh=mesh, in_specs=(row_spec, row_spec, row_spec, row_spec, replicated, replicated, replicated, replicated, expert_spec, expert_spec, expert_spec), out_specs=row_spec, check_vma=False)
```

profile of v0, /device:TPU:0, one launch (start us, length us, event | category | flops | bytes accessed | tf_op | source)
XLA Modules:
  0.0 554.7 jit_solution(2661181304414447990)
XLA Ops:
  0.0 1.3 compare_and_fusion.1
  1.4 0.0 copy-start.1
  1.4 0.1 copy.16
  1.5 0.2 reshape.60
  1.7 11.8 %scatter_custom_fusion = s32[6145]{0:T(1024)S(1)} fusion(s32[3072]{0:T(1024)S(1)} %bitcast.67, s32[3072]{0:T(1024)S(1)} %add_select_fusion, s32[]{:T(128)} %constant.39.clone.1), kind=kCustom, calls=%fused_computation.39 | custom fusion | bytes 24584 | tf_op jit(solution)/shard_map/scatter | solution.py:23
  13.6 35.4 %gather_fusion = bf16[6144,1280]{1,0:T(8,128)(2,1)} fusion(bf16[512,1280]{1,0:T(8,128)(2,1)} %param.11, s32[6144]{0:T(1024)S(1)} %get-tuple-element.8), kind=kCustom, calls=%fused_computation | custom fusion | bytes 31481856 | tf_op jit(solution)/shard_map/jit(_take)/gather | solution.py:24
  49.0 0.0 copy-done.1
  49.0 8.1 %broadcast_select_fusion = bf16[8,768,1280]{2,1,0:T(8,128)(2,1)S(1)} fusion(bf16[8,768,1280]{2,1,0:T(8,128)(2,1)} %bitcast.64, pred[8,768]{1,0:T(8,128)(4,1)S(1)} %compare_and_fusion), kind=kLoop, calls=%fused_computation.18 | loop fusion | flops 7864320 | bytes 31463424 | tf_op jit(solution)/shard_map/jit(_take)/select_n | solution.py:24
  57.1 176.7 %all_to_all.10 = bf16[8,768,1280]{2,1,0:T(8,128)(2,1)} all-to-all(bf16[8,768,1280]{2,1,0:T(8,128)(2,1)S(1)} %broadcast_select_fusion), channel_id=1, replica_groups=mesh['dp'=1,'ep'=8] {'ep'}, dimensions={0} | all-to-all | bytes 31457280 | tf_op jit(solution)/shard_map/all_to_all | solution.py:25
  233.8 27.6 %fusion.6 = f32[8,8,96,896]{3,2,1,0:T(8,128)} fusion(bf16[8,1280,896]{2,1,0:T(8,128)(2,1)} %param.20, bf16[8,8,96,1280]{3,2,1,0:T(8,128)(2,1)} %bitcast.65), kind=kOutput, calls=%fused_computation.13 | convolution fusion | flops 14092861440 | bytes 56098816 | tf_op jit(solution)/shard_map/secd,edf->secf/dot_general | solution.py:28
  261.4 40.2 %convert_bitcast_fusion = bf16[8,8,96,1280]{3,2,0,1:T(8,128)(2,1)} fusion(bf16[8,896,1280]{2,1,0:T(8,128)(2,1)} %param.21, f32[8,8,96,896]{3,2,1,0:T(8,128)} %fusion.6, bf16[8,1280,896]{2,1,0:T(8,128)(2,1)} %param.19, bf16[8,8,96,1280]{3,2,1,0:T(8,128)(2,1)} %bitcast.66), kind=kOutput, calls=%fused_computation.17 | convolution fusion | flops 28226617344 | bytes 90177536 | tf_op jit(solution)/shard_map/secf,efd->secd/dot_general | solution.py:30
  301.6 13.1 %copy.18 = bf16[8,8,96,1280]{3,2,1,0:T(8,128)(2,1)} copy(bf16[8,8,96,1280]{3,2,0,1:T(8,128)(2,1)} %convert_bitcast_fusion) | data formatting | bytes 31457280 | tf_op jit(solution)/shard_map/convert_element_type | solution.py:30
  314.8 0.0 copy-start.6
  314.8 0.0 copy-start
  314.8 4.7 all-to-all-start.1
  319.5 0.0 copy-done.2
  319.5 0.1 copy.19
  319.7 0.2 reshape.74
  319.9 0.0 copy-done.5
  319.9 0.2 copy.15
  320.1 0.0 copy-done.3
  320.1 0.0 copy-done.4
  320.1 0.1 copy.14
  320.2 0.0 copy-done.6
  320.3 0.0 copy-done
  320.3 0.4 fusion.36
  320.7 6.6 %fusion.37 = f32[512,1792]{1,0:T(8,128)} fusion(bf16[512,1280]{1,0:T(8,128)(2,1)S(1)} %copy-done, bf16[1280,1792]{1,0:T(8,128)(2,1)} %param.15), kind=kOutput, calls=%fused_computation.52 | convolution fusion | flops 2348810240 | bytes 9568256 | tf_op jit(solution)/shard_map/dot_general | solution.py:36
  327.4 164.7 %all-to-all-done.1 = bf16[8,768,1280]{2,1,0:T(8,128)(2,1)} async-done(((bf16[8,768,1280]{2,1,0:T(8,128)(2,1)}), bf16[8,768,1280]{2,1,0:T(8,128)(2,1)}, u32[]{:S(2)}, u32[]{:S(2)}) %all-to-all-start.1) | async-done | bytes 15728672 | tf_op jit(solution)/shard_map/all_to_all | solution.py:31
  492.0 25.0 %gather_fusion.1 = bf16[3072,1280]{1,0:T(8,128)(2,1)} fusion(bf16[6144,1280]{1,0:T(8,128)(2,1)} %bitcast.14, s32[3072]{0:T(1024)S(1)} %broadcast_clamp_fusion), kind=kCustom, calls=%fused_computation.1 | custom fusion | bytes 15740928 | tf_op jit(solution)/shard_map/jit(_take)/gather | solution.py:32
  517.0 13.0 %reshape.73 = bf16[512,6,1280]{2,1,0:T(8,128)(2,1)} reshape(bf16[3072,1280]{1,0:T(8,128)(2,1)} %gather_fusion.1) | data formatting | bytes 15728640 | tf_op jit(solution)/shard_map/jit(_take)/gather | solution.py:32
  530.1 13.0 %multiply_reduce_fusion = f32[512,1280]{1,0:T(8,128)} fusion(bf16[512,6,1280]{2,1,0:T(8,128)(2,1)} %reshape.73, f32[512,6]{1,0:T(8,128)S(1)} %copy.14, pred[512,6]{1,0:T(8,128)(4,1)S(1)} %copy.15), kind=kLoop, calls=%fused_computation.10 | loop fusion | flops 15073280 | bytes 10501120 | tf_op jit(solution)/shard_map/reduce_sum | solution.py:34
  543.1 11.6 %fusion.26 = bf16[512,1280]{1,0:T(8,128)(2,1)} fusion(f32[512,1280]{1,0:T(8,128)} %multiply_reduce_fusion, bf16[1792,1280]{1,0:T(8,128)(2,1)} %param.17, bf16[512,1280]{1,0:T(8,128)(2,1)S(1)} %copy-done, f32[512,1792]{1,0:T(8,128)} %fusion.37, bf16[1280,1792]{1,0:T(8,128)(2,1)} %param.16, f32[512]{0:T(512)S(1)} %add_divide_fusion), kind=kOutput, calls=%fused_computation.26 | convolution fusion | flops 4706402304 | bytes 18089984 | tf_op jit(solution)/shard_map/dot_general | solution.py:39
  (14 shorter events, 0.1 us)
Async XLA Ops:
  1.4 47.6 %copy-start.1 = (s32[512,6]{0,1:T(8,128)}, s32[512,6]{0,1:T(8,128)S(1)}, u32[]{:S(2)}) copy-start(s32[512,6]{0,1:T(8,128)S(1)} %get-tuple-element.6) | copy-start | bytes 36868
  314.7 4.8 copy-start.2
  314.7 5.1 copy-start.5
  314.8 5.3 copy-start.3
  314.8 5.3 copy-start.4
  314.8 5.5 copy-start.6
  314.8 5.5 copy-start
  314.8 177.3 %all-to-all-start.1 = ((bf16[8,768,1280]{2,1,0:T(8,128)(2,1)}), bf16[8,768,1280]{2,1,0:T(8,128)(2,1)}, u32[]{:S(2)}, u32[]{:S(2)}) async-start(bf16[8,768,1280]{2,1,0:T(8,128)(2,1)} %bitcast.63), calls=%async_computation.1 | async-start | bytes 31457280 | tf_op jit(solution)/shard_map/all_to_all | solution.py:31
where the time goes:
time: 555 us
  blocking collectives  177 us (32%)
  waiting for transfers between devices  165 us (30%)
  local copies, waits for them, and re-layouts  99.4 us (18%)
  matrix products  86.4 us (16%)
  other arithmetic  22.5 us (4%)
    all_to_all x1, blocking collectives, device_step(): lax.all_to_all(send_buf.reshape(num_ep, local_experts * capacity, hidden)...  177 us
    all_to_all x1, waiting for transfers between devices, device_step(): lax.all_to_all(expert_out.reshape(num_ep, local_experts * capacity, hidde...  165 us
    dot_general x1, matrix products, device_step(): jnp.einsum('secf,efd->secd', hidden_act, expert_w2, preferred_element_typ...  40.2 us
    gather x2, local copies, waits for them, and re-layouts, device_step(): jnp.take(back_buf.reshape(buf_rows, hidden), slot_dest, axis=0, mode='fil...  38 us
    gather x1, local copies, waits for them, and re-layouts, device_step(): jnp.take(tokens, row_owner[:buf_rows], axis=0, mode='fill', fill_value=0)  35.4 us
    dot_general x1, matrix products, device_step(): jnp.einsum('secd,edf->secf', expert_in, expert_w3, preferred_element_type...  27.6 us
    convert_element_type x1, local copies, waits for them, and re-layouts, device_step(): jnp.einsum('secf,efd->secd', hidden_act, expert_w2, preferred_element_typ...  13.1 us
    reduce_sum x1, other arithmetic, device_step(): routed = jnp.sum(weights * picked, axis=1)  13 us
  transfers between devices with their start and end apart: 1, of which 1 were waited for; matrix products, arithmetic and copies ran while one was open for 1% of the time, Pallas kernels for 0%

commit v1 on v0

v1 whole, which is shorter than its diff:
```python
import functools

import jax
import jax.numpy as jnp
from jax import lax
from jax.experimental import pallas as pl
from jax.experimental.pallas import tpu as pltpu
from jax.sharding import PartitionSpec as P

SLOTS = 3
CHUNK = 128
f32, bf16 = jnp.float32, jnp.bfloat16


def dot(a, b):
    return jnp.dot(a, b, preferred_element_type=f32)


def moe_kernel(num_ep, local, cap, top_k, meta_ref, tok_ref, gate_ref, sw1, sw3, sw2, ew1, ew3, ew2, out_ref,
               meta_all, tb, r_mine, r_out, r_in, w1s, w3s, w2s, acc, s1, sd, got1, gotd, got2, h_ref, xs, gm,
               w_sem, m_send, m_recv, t_send, t_recv, r_send, r_recv, s_send, s_recv):
    tok_count, hidden = tok_ref.shape
    ff = w1s.shape[2]
    rows = local * cap
    chunks = tok_count // CHUNK
    me = lax.axis_index('ep')
    core, xx, yy = me % 2, (me // 2) % 2, me // 4
    step_x, step_y = 2 - 4 * xx, 4 - 8 * yy
    part = me + 1 - 2 * core
    off1 = (1 - core) * step_x + core * step_y
    off2 = core * step_x + (1 - core) * step_y
    n1, n2, diag = me + off1, me + off2, me + step_x + step_y
    pn1, pn2, pdiag = part + off2, part + off1, part + step_x + step_y

    def remote(src, dst, ss, rs, dev):
        return pltpu.make_async_remote_copy(src_ref=src, dst_ref=dst, send_sem=ss, recv_sem=rs,
                                            device_id={'ep': dev}, device_id_type=pl.DeviceIdType.MESH)

    def weight_copies(src1, src3, src2, slot):
        return [pltpu.make_async_copy(src1, w1s.at[slot], w_sem.at[slot, 0]),
                pltpu.make_async_copy(src3, w3s.at[slot], w_sem.at[slot, 1]),
                pltpu.make_async_copy(src2, w2s.at[slot], w_sem.at[slot, 2])]

    def start_expert(e, slot):
        for c in weight_copies(ew1.at[e], ew3.at[e], ew2.at[e], slot):
            c.start()

    def wait_weights(slot):
        for c in weight_copies(ew1.at[0], ew3.at[0], ew2.at[0], slot):
            c.wait()

    for s in range(2):
        cols = pl.ds(s * ff, ff)
        for c in weight_copies(sw1.at[:, cols], sw3.at[:, cols], sw2.at[cols, :], s):
            c.start()
    start_expert(0, 2)

    barrier = pltpu.get_barrier_semaphore()
    for k in range(1, num_ep):
        pl.semaphore_signal(barrier, inc=1, device_id={'ep': (me + k) % num_ep}, device_id_type=pl.DeviceIdType.MESH)
    pl.semaphore_wait(barrier, num_ep - 1)

    meta_copies = [remote(meta_ref, meta_all.at[me], m_send.at[k - 1], m_recv.at[k - 1], (me + k) % num_ep) for k in range(1, num_ep)]
    for c in meta_copies:
        c.start()
    t_own = remote(tok_ref, tb.at[0], t_send.at[0], t_recv.at[0], part)
    t_n1 = remote(tok_ref, tb.at[1], t_send.at[1], t_recv.at[1], n1)
    t_n1p = remote(tb.at[1], tb.at[2], t_send.at[2], t_recv.at[2], part)
    t_d = remote(tb.at[1], tb.at[3], t_send.at[3], t_recv.at[3], n2)
    t_dp = remote(tb.at[3], tb.at[4], t_send.at[4], t_recv.at[4], part)
    t_n2 = remote(tok_ref, tb.at[5], t_send.at[5], t_recv.at[5], n2)
    t_n2p = remote(tb.at[5], tb.at[6], t_send.at[6], t_recv.at[6], part)
    t_n1.start()
    t_own.start()
    meta_all[me] = meta_ref[...]

    def swiglu_up(x, slot, put):
        full = ff // 256
        for c in range(full):
            cols = slice(c * 256, c * 256 + 256)
            a = dot(x, w1s[slot, :, cols])
            b = dot(x, w3s[slot, :, cols])
            put(cols, (jax.nn.silu(a) * b).astype(bf16))
        cols = slice(full * 256, ff)
        rest = ff - full * 256
        ab = dot(x, jnp.concatenate([w1s[slot, :, cols], w3s[slot, :, cols]], axis=1))
        put(cols, (jax.nn.silu(ab[:, :rest]) * ab[:, rest:]).astype(bf16))

    mrows = 256

    def shared_half(s):
        wait_weights(s)

        def block(i, _):
            rs = pl.ds(pl.multiple_of(i * mrows, mrows), mrows)

            def put(cols, v):
                h_ref[rs, cols] = v
            swiglu_up(tok_ref[rs, :], s, put)
            if s == 1:
                logit = jnp.sum(tok_ref[rs, :].astype(f32) * gate_ref[...].astype(f32), axis=1, keepdims=True)
                sig = jax.nn.sigmoid(logit)
            for n in range(hidden // 256):
                cols = slice(n * 256, n * 256 + 256)
                v = dot(h_ref[rs, :], w2s[s, :, cols])
                if s == 0:
                    acc[rs, cols] = v
                else:
                    acc[rs, cols] = tok_ref[rs, cols].astype(f32) + sig * (acc[rs, cols] + v)
            return 0
        lax.fori_loop(0, tok_count // mrows, block, 0)
        start_expert(s + 1, s)

    shared_half(0)
    shared_half(1)
    for c in meta_copies:
        c.wait()

    t_n1.wait_recv()
    t_d.start()
    t_n1p.start()
    t_n2.start()
    t_n1p.wait_recv()

    lane_row = lax.broadcasted_iota(jnp.int32, (cap, tok_count), 0).astype(f32)
    lane_col = lax.broadcasted_iota(jnp.int32, (CHUNK, 128), 1).astype(f32)

    def expert_loop(p, mine, other, src, psrc):
        par = p % 2

        def body(e, _):
            slot = (p * local + 2 + e) % SLOTS
            base = ((me * local + e) * cap).astype(f32)
            for u, (unit, who) in enumerate(((mine, src), (other, psrc))):
                d = meta_all[who, 0:8, :] - base
                hit = d[0:1, :] == lane_row
                for k in range(1, top_k):
                    hit = hit | (d[k:k + 1, :] == lane_row)
                pick = jnp.where(hit, 1.0, 0.0).astype(bf16)
                for n in range(hidden // 256):
                    cols = slice(n * 256, n * 256 + 256)
                    xs[u * cap:(u + 1) * cap, cols] = dot(pick, unit[:, cols]).astype(bf16)
            wait_weights(slot)

            def put(cols, v):
                h_ref[0:2 * cap, cols] = v
            swiglu_up(xs[...], slot, put)
            rs = pl.ds(pl.multiple_of(e * cap, cap), cap)
            for n in range(hidden // 256):
                cols = slice(n * 256, n * 256 + 256)
                v = dot(h_ref[0:2 * cap, :], w2s[slot, :, cols]).astype(bf16)
                r_mine[rs, cols] = v[:cap]
                r_out[rs, cols] = v[cap:]
            remote(r_out.at[rs], r_in.at[par, rs], r_send, r_recv.at[par], part).start()
            if p < 3:
                start_expert((e + SLOTS) % local, slot)
            else:
                @pl.when(e + SLOTS < local)
                def _():
                    start_expert(e + SLOTS, slot)
            return 0
        lax.fori_loop(0, local, body, 0)

    def combine(p, src, store, send):
        par = p % 2
        whole = remote(r_out, r_in.at[par], r_send, r_recv.at[par], part)
        whole.wait()
        nr = rows // 128

        def block(i, _):
            rs = pl.ds(pl.multiple_of(i * CHUNK, CHUNK), CHUNK)
            m = jnp.transpose(meta_all[src, :, rs])
            for half, owner in enumerate((me, part)):
                base = (owner * rows).astype(f32)
                for c in range(nr):
                    rid = lane_col + (base + c * 128.0)
                    g = jnp.where(m[:, 0:1] == rid, m[:, 8:9], 0.0)
                    for k in range(1, top_k):
                        g = jnp.where(m[:, k:k + 1] == rid, m[:, 8 + k:9 + k], g)
                    g1 = g.astype(bf16)
                    rem = g - g1.astype(f32)
                    g2 = rem.astype(bf16)
                    g3 = (rem - g2.astype(f32)).astype(bf16)
                    lanes = slice(half * rows + c * 128, half * rows + c * 128 + 128)
                    gm[0, :, lanes] = g1
                    gm[1, :, lanes] = g2
                    gm[2, :, lanes] = g3
            for n in range(hidden // 256):
                cols = slice(n * 256, n * 256 + 256)
                v = None
                for q in range(3):
                    t = dot(gm[q, :, 0:rows], r_mine[:, cols]) + dot(gm[q, :, rows:], r_in[par, :, cols])
                    v = t if v is None else v + t
                store(rs, cols, v + v)
            send(i, rs)
            return 0
        lax.fori_loop(0, chunks, block, 0)

    def chunk_rows(c):
        return pl.ds(c * CHUNK, CHUNK)

    def put_s1(rs, cols, v):
        s1[rs, cols] = v

    def put_sd(rs, cols, v):
        sd[rs, cols] = v

    def put_acc(rs, cols, v):
        acc[rs, cols] = acc[rs, cols] + v

    def s_copy(which, src, dst, c, rs, dev):
        return remote(src.at[rs], dst.at[rs], s_send.at[which, c], s_recv.at[which, c], dev)

    def no_send(i, rs):
        pass

    expert_loop(0, tb.at[1], tb.at[2], n1, pn1)
    t_d.wait_recv()
    t_dp.start()
    combine(0, n1, put_s1, lambda i, rs: s_copy(0, s1, got1, i, rs, n1).start())
    t_dp.wait_recv()

    expert_loop(1, tb.at[3], tb.at[4], diag, pdiag)
    t_n2.wait_recv()
    t_n2p.start()
    combine(1, diag, put_sd, lambda i, rs: s_copy(1, sd, gotd, i, rs, n1).start())
    t_n2p.wait_recv()

    expert_loop(2, tb.at[5], tb.at[6], n2, pn2)
    for c in range(chunks):
        s_copy(0, s1, got1, c, chunk_rows(c), n1).wait_send()
    combine(2, n2, put_s1, no_send)
    t_own.wait_recv()

    expert_loop(3, tok_ref, tb.at[0], me, part)
    combine(3, me, put_acc, no_send)

    for c in range(chunks):
        rs = chunk_rows(c)
        s_copy(1, sd, gotd, c, rs, n1).wait_recv()
        s1[rs, :] = s1[rs, :] + gotd[rs, :]
        s_copy(2, s1, got2, c, rs, n2).start()
    for c in range(chunks):
        rs = chunk_rows(c)
        s_copy(0, s1, got1, c, rs, n1).wait_recv()
        s_copy(2, s1, got2, c, rs, n2).wait_recv()
        out_ref[rs, :] = (acc[rs, :] + got1[rs, :] + got2[rs, :]).astype(bf16)
    for c in range(chunks):
        rs = chunk_rows(c)
        s_copy(1, sd, gotd, c, rs, n1).wait_send()
        s_copy(2, s1, got2, c, rs, n2).wait_send()
    for t in (t_own, t_n1, t_n1p, t_d, t_dp, t_n2, t_n2p):
        t.wait_send()


def solution(mesh):
    num_ep = mesh.shape['ep']
    row_spec = P(('dp', 'ep'), None)
    replicated = P()
    expert_spec = P('ep', None, None)

    def device_step(tokens, expert_ids, gate_vals, slots, shared_w1, shared_w3, shared_w2, shared_gate, expert_w1, expert_w3, expert_w2):
        tok_count, hidden = tokens.shape
        top_k = expert_ids.shape[1]
        local, _, ff = expert_w1.shape
        num_experts = local * num_ep
        cap = 8 * ((2 * tok_count * top_k + 8 * num_experts - 1) // (8 * num_experts))
        rows = local * cap
        chunks = tok_count // CHUNK
        kept = slots >= 0
        dest = jnp.where(kept, expert_ids * cap + slots, -1).astype(f32)
        pad = ((0, 8 - top_k), (0, 0))
        meta = jnp.concatenate([jnp.pad(dest.T, pad, constant_values=-1.0), jnp.pad(jnp.where(kept, 0.5 * gate_vals, 0.0).T, pad)], axis=0)
        vm = pl.BlockSpec(memory_space=pltpu.VMEM)
        hbm = pl.BlockSpec(memory_space=pltpu.HBM)
        dma = pltpu.SemaphoreType.DMA
        return pl.pallas_call(
            functools.partial(moe_kernel, num_ep, local, cap, top_k),
            out_shape=jax.ShapeDtypeStruct((tok_count, hidden), bf16),
            in_specs=[vm, vm, vm] + [hbm] * 6,
            out_specs=vm,
            scratch_shapes=[
                pltpu.VMEM((num_ep, 16, tok_count), f32),
                pltpu.VMEM((7, tok_count, hidden), bf16),
                pltpu.VMEM((rows, hidden), bf16),
                pltpu.VMEM((rows, hidden), bf16),
                pltpu.VMEM((2, rows, hidden), bf16),
                pltpu.VMEM((SLOTS, hidden, ff), bf16),
                pltpu.VMEM((SLOTS, hidden, ff), bf16),
                pltpu.VMEM((SLOTS, ff, hidden), bf16),
            ] + [pltpu.VMEM((tok_count, hidden), f32)] * 6 + [
                pltpu.VMEM((tok_count, ff), bf16),
                pltpu.VMEM((2 * cap, hidden), bf16),
                pltpu.VMEM((3, CHUNK, 2 * rows), bf16),
                dma((SLOTS, 3)), dma((num_ep - 1,)), dma((num_ep - 1,)), dma((7,)), dma((7,)),
                dma, dma((2,)), dma((3, chunks)), dma((3, chunks)),
            ],
            compiler_params=pltpu.CompilerParams(collective_id=0, has_side_effects=True, vmem_limit_bytes=67043328),
        )(meta, tokens, shared_gate.reshape(1, hidden), shared_w1, shared_w3, shared_w2, expert_w1, expert_w3, expert_w2)

    return jax.shard_map(device_step, mesh=mesh, in_specs=(row_spec, row_spec, row_spec, row_spec, replicated, replicated, replicated, replicated, expert_spec, expert_spec, expert_spec), out_specs=row_spec, check_vma=False)
```

time: 555 us -> 183 us (0.33)
  Pallas kernels: 0 us -> 177 us
  blocking collectives: 177 us -> 0 us
  waiting for transfers between devices: 165 us -> 0 us
  local copies, waits for them, and re-layouts: 99.4 us -> 3.74 us
  matrix products: 86.4 us -> 0 us
  other arithmetic: 22.5 us -> 2.1 us
    pallas_call x0 -> x1, Pallas kernels: none -> 177 us  [device_step(): pl.pallas_call(functools.partial(moe_kernel, num_ep, local, cap, top_k),...]
    all_to_all x1 -> x0, blocking collectives: 177 us -> none  [device_step(): lax.all_to_all(send_buf.reshape(num_ep, local_experts * capacity, hidden)...]
    all_to_all x1 -> x0, waiting for transfers between devices: 165 us -> none  [device_step(): lax.all_to_all(expert_out.reshape(num_ep, local_experts * capacity, hidde...]
    dot_general x5 -> x0, matrix products: 86.4 us -> none  [the longest x1 40.2 us: device_step(): jnp.einsum('secf,efd->secd', hidden_act, expert_w2, preferred_element_typ...]
    gather x3 -> x0, local copies, waits for them, and re-layouts: 73.4 us -> none  [the longest x2 38 us: device_step(): jnp.take(back_buf.reshape(buf_rows, hidden), slot_dest, axis=0, mode='fil...]
    convert_element_type x1 -> x0, local copies, waits for them, and re-layouts: 13.1 us -> none  [device_step(): jnp.einsum('secf,efd->secd', hidden_act, expert_w2, preferred_element_typ...]
    reduce_sum x1 -> x0, other arithmetic: 13 us -> none  [device_step(): routed = jnp.sum(weights * picked, axis=1)]
    scatter x1 -> x0, local copies, waits for them, and re-layouts: 11.8 us -> none  [device_step(): jnp.full((buf_rows + 1,), tok_count, jnp.int32).at[slot_dest.reshape(-1)]]
  transfers between devices with their start and end apart: 1 -> 0, of which waited for: 1 -> 0; matrix products, arithmetic and copies ran while one was open for 1% -> 0% of each run, Pallas kernels for 0% -> 0%
where the time goes in v1:
time: 183 us
  Pallas kernels  177 us (97%)
  local copies, waits for them, and re-layouts  3.74 us (2%)
  other arithmetic  2.1 us (1%)
    pallas_call x1, Pallas kernels, device_step(): pl.pallas_call(functools.partial(moe_kernel, num_ep, local, cap, top_k),...  177 us

profile of v1, /device:TPU:0, one launch (start us, length us, event | category | flops | bytes accessed | tf_op | source)
XLA Modules:
  0.0 182.9 jit_solution(12374620248099150947)
XLA Ops:
  0.0 1.3 reshape.3.gate_ref
  1.3 0.7 convert_bitcast_fusion
  2.0 0.7 select_bitcast_fusion
  2.8 0.6 select_maximum_fusion.meta_ref
  3.4 177.1 %shard_map.109 = bf16[512,1280]{1,0:T(8,128)(2,1)} custom-call(f32[16,512]{1,0:T(8,128)} %select_maximum_fusion.meta_ref, bf16[512,1280]{1,0:T(8,128)(2,1)} %tok_ref.1, bf16[1,1280]{1,0:T(2,128)(2,1)} %reshape.3.gate_ref, bf16[1280,1792]{1,0:T(8,128)(2,1)} %sw1.1, bf16[1280,1792]{1,0:T(8,128)(2,1)} %sw3.1, bf16[1792,1280]{1,0:T(8,128)(2,1)} %sw2.1, ...), custom_call_target="tpu_custom_call" | custom-call | tf_op jit(solution)/shard_map/pallas_call | solution.py:277
  180.5 2.5 %copy.13 = bf16[512,1280]{1,0:T(8,128)(2,1)} copy(bf16[512,1280]{1,0:T(8,128)(2,1)} %shard_map.109) | data formatting | bytes 2621440

commit v2 on v1

v2 whole, which is shorter than its diff:
```python
import functools

import jax
import jax.numpy as jnp
from jax import lax
from jax.experimental import pallas as pl
from jax.experimental.pallas import tpu as pltpu
from jax.sharding import PartitionSpec as P

SLOTS = 3
CHUNK = 128
f32, bf16 = jnp.float32, jnp.bfloat16


def dot(a, b):
    return jnp.dot(a, b, preferred_element_type=f32)


def moe_kernel(num_ep, local, cap, top_k, ids_ref, slot_ref, gval_ref, tok_ref, gate_ref, sw1, sw3, sw2, ew1, ew3, ew2, out_ref,
               tb, mb, r_mine, r_out, r_in, w1s, w3s, w2s, s1, sd, got1, gotd, got2, h_ref, xs, gma, gmb,
               w_sem, t_send, t_recv, m_send, m_recv, r_send, r_recv, s_send, s_recv):
    tok_count, hidden = tok_ref.shape
    ff = w1s.shape[2]
    rows = local * cap
    chunks = tok_count // CHUNK
    me = lax.axis_index('ep')
    core, xx, yy = me % 2, (me // 2) % 2, me // 4
    step_x, step_y = 2 - 4 * xx, 4 - 8 * yy
    part = me + 1 - 2 * core
    n1 = me + (1 - core) * step_x + core * step_y
    n2 = me + core * step_x + (1 - core) * step_y

    def remote(src, dst, ss, rs, dev):
        return pltpu.make_async_remote_copy(src_ref=src, dst_ref=dst, send_sem=ss, recv_sem=rs,
                                            device_id={'ep': dev}, device_id_type=pl.DeviceIdType.MESH)

    def weight_copies(src1, src3, src2, slot):
        return [pltpu.make_async_copy(src1, w1s.at[slot], w_sem.at[slot, 0]),
                pltpu.make_async_copy(src3, w3s.at[slot], w_sem.at[slot, 1]),
                pltpu.make_async_copy(src2, w2s.at[slot], w_sem.at[slot, 2])]

    def start_expert(e, slot):
        for c in weight_copies(ew1.at[e], ew3.at[e], ew2.at[e], slot):
            c.start()

    def start_shared(s, slot):
        cols = pl.ds(s * ff, ff)
        for c in weight_copies(sw1.at[:, cols], sw3.at[:, cols], sw2.at[cols, :], slot):
            c.start()

    def wait_weights(slot):
        for c in weight_copies(ew1.at[0], ew3.at[0], ew2.at[0], slot):
            c.wait()

    for e in range(SLOTS):
        start_expert(e, e)

    kept = slot_ref[...] >= 0
    mb[7, 0:top_k, :] = jnp.where(kept, ids_ref[...] * cap + slot_ref[...], -1).astype(f32)
    mb[7, top_k:8, :] = jnp.full((8 - top_k, tok_count), -1.0, f32)
    mb[7, 8:8 + top_k, :] = jnp.where(kept, 0.5 * gval_ref[...], 0.0)
    mb[7, 8 + top_k:16, :] = jnp.zeros((8 - top_k, tok_count), f32)

    barrier = pltpu.get_barrier_semaphore()
    for k in range(1, num_ep):
        pl.semaphore_signal(barrier, inc=1, device_id={'ep': (me + k) % num_ep}, device_id_type=pl.DeviceIdType.MESH)
    pl.semaphore_wait(barrier, num_ep - 1)

    class Hop:
        def __init__(self, src, dst, dev):
            self.copies = (remote(mb.at[src], mb.at[dst], m_send.at[dst], m_recv.at[dst], dev),
                           remote(tok_ref if src == 7 else tb.at[src], tb.at[dst], t_send.at[dst], t_recv.at[dst], dev))

        def start(self):
            for c in self.copies:
                c.start()

        def wait_recv(self):
            for c in self.copies:
                c.wait_recv()

        def wait_send(self):
            for c in self.copies:
                c.wait_send()

    t_own, t_n1, t_n1p, t_d, t_dp, t_n2, t_n2p = (
        Hop(7, 0, part), Hop(7, 1, n1), Hop(1, 2, part), Hop(1, 3, n2), Hop(3, 4, part), Hop(7, 5, n2), Hop(5, 6, part))
    t_n1.start()
    t_own.start()

    def swiglu_up(x, slot, put):
        full = ff // 256
        for c in range(full):
            cols = slice(c * 256, c * 256 + 256)
            a = dot(x, w1s[slot, :, cols])
            b = dot(x, w3s[slot, :, cols])
            put(cols, (jax.nn.silu(a) * b).astype(bf16))
        cols = slice(full * 256, ff)
        rest = ff - full * 256
        ab = dot(x, jnp.concatenate([w1s[slot, :, cols], w3s[slot, :, cols]], axis=1))
        put(cols, (jax.nn.silu(ab[:, :rest]) * ab[:, rest:]).astype(bf16))

    lane_row = lax.broadcasted_iota(jnp.int32, (cap, tok_count), 0).astype(f32)
    lane_col = lax.broadcasted_iota(jnp.int32, (CHUNK, 128), 1).astype(f32)

    def whole_rows(par):
        return remote(r_out, r_in.at[par], r_send, r_recv.at[par], part)

    def expert_loop(order, par, keep, mine, other, mi, oi, late=None):
        def dispatch(e):
            base = ((me * local + e) * cap).astype(f32)
            for u, (unit, who) in enumerate(((mine, mi), (other, oi))):
                d = mb[who, 0:8, :] - base
                hit = d[0:1, :] == lane_row
                for k in range(1, top_k):
                    hit = hit | (d[k:k + 1, :] == lane_row)
                pick = jnp.where(hit, 1.0, 0.0).astype(bf16)
                for n in range(hidden // 256):
                    cols = slice(n * 256, n * 256 + 256)
                    xs[u * cap:(u + 1) * cap, cols] = dot(pick, unit[:, cols]).astype(bf16)

        dispatch(jnp.int32(0))

        def body(e, _):
            if late is not None:
                pl.when(e == local - 1)(late)
            slot = (order * local + e) % SLOTS
            wait_weights(slot)

            def put(cols, v):
                h_ref[0:2 * cap, cols] = v
            swiglu_up(xs[...], slot, put)
            dispatch(e + 1)
            rs = pl.ds(pl.multiple_of(e * cap, cap), cap)
            for n in range(hidden // 256):
                cols = slice(n * 256, n * 256 + 256)
                v = dot(h_ref[0:2 * cap, :], w2s[slot, :, cols]).astype(bf16)
                r_mine[keep, rs, cols] = v[:cap]
                r_out[rs, cols] = v[cap:]
            remote(r_out.at[rs], r_in.at[par, rs], r_send, r_recv.at[par], part).start()
            if order < 3:
                start_expert((e + SLOTS) % local, slot)
            else:
                @pl.when(e + SLOTS < local)
                def _():
                    start_expert(e + SLOTS, slot)
                for s in range(2):
                    @pl.when(e + SLOTS == local + s)
                    def _():
                        start_shared(s, slot)
            return 0
        lax.fori_loop(0, local, body, 0)

    def combine(par, keep, mi, ready, store, send, wait_rows):
        nr = rows // 128

        def build(i, gm):
            rs = pl.ds(pl.multiple_of(i * CHUNK, CHUNK), CHUNK)
            m = jnp.transpose(mb[mi, :, rs])
            for half, owner in enumerate((me, part)):
                base = (owner * rows).astype(f32)
                for c in range(nr):
                    rid = lane_col + (base + c * 128.0)
                    g = jnp.where(m[:, 0:1] == rid, m[:, 8:9], 0.0)
                    for k in range(1, top_k):
                        g = jnp.where(m[:, k:k + 1] == rid, m[:, 8 + k:9 + k], g)
                    g1 = g.astype(bf16)
                    rem = g - g1.astype(f32)
                    g2 = rem.astype(bf16)
                    g3 = (rem - g2.astype(f32)).astype(bf16)
                    lanes = slice(half * rows + c * 128, half * rows + c * 128 + 128)
                    gm[0, :, lanes] = g1
                    gm[1, :, lanes] = g2
                    gm[2, :, lanes] = g3

        def products(i, gm):
            rs = pl.ds(pl.multiple_of(i * CHUNK, CHUNK), CHUNK)
            for n in range(hidden // 256):
                cols = slice(n * 256, n * 256 + 256)
                v = None
                for q in range(3):
                    t = dot(gm[q, :, 0:rows], r_mine[keep, :, cols]) + dot(gm[q, :, rows:], r_in[par, :, cols])
                    v = t if v is None else v + t
                store(rs, cols, v + v)

        build(jnp.int32(0), gma)
        wait_rows()

        def pair(j, _):
            for t, (now, later) in enumerate(((gma, gmb), (gmb, gma))):
                i = 2 * j + t
                rs = pl.ds(pl.multiple_of(i * CHUNK, CHUNK), CHUNK)
                ready(i, rs)
                build((i + 1) % chunks, later)
                products(i, now)
                send(i, rs)
            return 0
        lax.fori_loop(0, chunks // 2, pair, 0)

    def chunk_rows(c):
        return pl.ds(c * CHUNK, CHUNK)

    def s_copy(which, c, rs):
        src, dst, dev = ((s1, got1, n1), (sd, gotd, n1), (s1, got2, n2))[which]
        return remote(src.at[rs], dst.at[rs], s_send.at[which, c], s_recv.at[which, c], dev)

    def put_s1(rs, cols, v):
        s1[rs, cols] = v

    def put_sd(rs, cols, v):
        sd[rs, cols] = v

    def put_s2(rs, cols, v):
        s1[rs, cols] = v + gotd[rs, cols]

    def nothing(i, rs):
        pass

    def first_tokens():
        t_n1.wait_recv()
        t_d.start()
        t_n1p.start()
        t_n2.start()

    t_own.wait_recv()
    expert_loop(0, 2, 1, tok_ref, tb.at[0], 7, 0, late=first_tokens)
    t_n1p.wait_recv()
    whole_rows(2).wait_send()

    expert_loop(1, 0, 0, tb.at[1], tb.at[2], 1, 2)
    t_d.wait_recv()
    t_dp.start()
    combine(0, 0, 1, nothing, put_s1, lambda i, rs: s_copy(0, i, rs).start(), lambda: whole_rows(0).wait())
    t_dp.wait_recv()

    expert_loop(2, 1, 0, tb.at[3], tb.at[4], 3, 4)
    t_n2.wait_recv()
    t_n2p.start()
    combine(1, 0, 3, nothing, put_sd, lambda i, rs: s_copy(1, i, rs).start(), lambda: whole_rows(1).wait())
    t_n2p.wait_recv()

    expert_loop(3, 0, 0, tb.at[5], tb.at[6], 5, 6)
    for c in range(chunks):
        s_copy(0, c, chunk_rows(c)).wait_send()
    combine(0, 0, 5, lambda i, rs: s_copy(1, i, rs).wait_recv(), put_s2, lambda i, rs: s_copy(2, i, rs).start(),
            lambda: whole_rows(0).wait())

    for c in range(chunks):
        s_copy(1, c, chunk_rows(c)).wait_send()
    combine(2, 1, 7, nothing, put_sd, nothing, lambda: whole_rows(2).wait_recv())

    mrows = 256
    for s in range(2):
        slot = (4 * local + s) % SLOTS
        wait_weights(slot)

        def block(i, _):
            rs = pl.ds(pl.multiple_of(i * mrows, mrows), mrows)

            def put(cols, v):
                h_ref[:, cols] = v
            swiglu_up(tok_ref[rs, :], slot, put)
            logit = jnp.sum(tok_ref[rs, :].astype(f32) * gate_ref[...].astype(f32).reshape(1, hidden), axis=1, keepdims=True)
            sig = jax.nn.sigmoid(logit)
            for n in range(hidden // 256):
                cols = slice(n * 256, n * 256 + 256)
                v = sd[rs, cols] + sig * dot(h_ref[...], w2s[slot, :, cols])
                if s == 1:
                    v = v + tok_ref[rs, cols].astype(f32)
                sd[rs, cols] = v
            return 0
        lax.fori_loop(0, tok_count // mrows, block, 0)

    for c in range(chunks):
        rs = chunk_rows(c)
        s_copy(0, c, rs).wait_recv()
        s_copy(2, c, rs).wait_recv()
        out_ref[rs, :] = (sd[rs, :] + got1[rs, :] + got2[rs, :]).astype(bf16)
    for c in range(chunks):
        s_copy(2, c, chunk_rows(c)).wait_send()
    for t in (t_own, t_n1, t_n1p, t_d, t_dp, t_n2, t_n2p):
        t.wait_send()


def solution(mesh):
    num_ep = mesh.shape['ep']
    row_spec = P(('dp', 'ep'), None)
    replicated = P()
    expert_spec = P('ep', None, None)

    def device_step(tokens, expert_ids, gate_vals, slots, shared_w1, shared_w3, shared_w2, shared_gate, expert_w1, expert_w3, expert_w2):
        tok_count, hidden = tokens.shape
        top_k = expert_ids.shape[1]
        local, _, ff = expert_w1.shape
        num_experts = local * num_ep
        cap = 8 * ((2 * tok_count * top_k + 8 * num_experts - 1) // (8 * num_experts))
        rows = local * cap
        chunks = tok_count // CHUNK
        vm = pl.BlockSpec(memory_space=pltpu.VMEM)
        hbm = pl.BlockSpec(memory_space=pltpu.HBM)
        dma = pltpu.SemaphoreType.DMA
        return pl.pallas_call(
            functools.partial(moe_kernel, num_ep, local, cap, top_k),
            out_shape=jax.ShapeDtypeStruct((tok_count, hidden), bf16),
            in_specs=[vm] * 5 + [hbm] * 6,
            out_specs=vm,
            scratch_shapes=[
                pltpu.VMEM((7, tok_count, hidden), bf16),
                pltpu.VMEM((8, 16, tok_count), f32),
                pltpu.VMEM((2, rows, hidden), bf16),
                pltpu.VMEM((rows, hidden), bf16),
                pltpu.VMEM((3, rows, hidden), bf16),
                pltpu.VMEM((SLOTS, hidden, ff), bf16),
                pltpu.VMEM((SLOTS, hidden, ff), bf16),
                pltpu.VMEM((SLOTS, ff, hidden), bf16),
            ] + [pltpu.VMEM((tok_count, hidden), f32)] * 5 + [
                pltpu.VMEM((256, ff), bf16),
                pltpu.VMEM((2 * cap, hidden), bf16),
                pltpu.VMEM((3, CHUNK, 2 * rows), bf16),
                pltpu.VMEM((3, CHUNK, 2 * rows), bf16),
                dma((SLOTS, 3)), dma((7,)), dma((7,)), dma((7,)), dma((7,)),
                dma, dma((3,)), dma((3, chunks)), dma((3, chunks)),
            ],
            compiler_params=pltpu.CompilerParams(collective_id=0, has_side_effects=True, vmem_limit_bytes=67043328),
        )(expert_ids.T, slots.T, gate_vals.T, tokens, shared_gate, shared_w1, shared_w3, shared_w2, expert_w1, expert_w3, expert_w2)

    return jax.shard_map(device_step, mesh=mesh, in_specs=(row_spec, row_spec, row_spec, row_spec, replicated, replicated, replicated, replicated, expert_spec, expert_spec, expert_spec), out_specs=row_spec, check_vma=False)
```

time: 183 us -> 143 us (0.78)
  Pallas kernels: 177 us -> 140 us
  other arithmetic: 2.1 us -> 0 us
    pallas_call x1, Pallas kernels: 177 us -> 140 us  [device_step(): pl.pallas_call(functools.partial(moe_kernel, num_ep, local, cap, top_k),...]
where the time goes in v2:
time: 143 us
  Pallas kernels  140 us (98%)
  local copies, waits for them, and re-layouts  2.46 us (2%)
    pallas_call x1, Pallas kernels, device_step(): pl.pallas_call(functools.partial(moe_kernel, num_ep, local, cap, top_k),...  140 us

profile of v2, /device:TPU:0, one launch (start us, length us, event | category | flops | bytes accessed | tf_op | source)
XLA Modules:
  0.0 142.6 jit_solution(14893759346081864166)
XLA Ops:
  0.0 140.2 %shard_map.109 = bf16[512,1280]{1,0:T(8,128)(2,1)} custom-call(s32[6,512]{1,0:T(8,128)} %bitcast.3, s32[6,512]{1,0:T(8,128)} %bitcast.4, f32[6,512]{1,0:T(8,128)} %bitcast.5, bf16[512,1280]{1,0:T(8,128)(2,1)} %tok_ref.1, bf16[1280]{0:T(1024)(128)(2,1)} %gate_ref.1, bf16[1280,1792]{1,0:T(8,128)(2,1)} %sw1.1, bf16[1280,1792]{1,0:T(8,128)(2,1)} %sw3.1, ...), custom_call_target="tpu_custom_call" | custom-call | tf_op jit(solution)/shard_map/pallas_call | solution.py:302
  140.2 2.5 %copy.13 = bf16[512,1280]{1,0:T(8,128)(2,1)} copy(bf16[512,1280]{1,0:T(8,128)(2,1)} %shard_map.109) | data formatting | bytes 2621440

commit v3 on v2

--- a/solution.py
+++ b/solution.py
@@ -9,6 +9,7 @@
 
 SLOTS = 3
 CHUNK = 128
+HEAD = 256
 f32, bf16 = jnp.float32, jnp.bfloat16
 
 
@@ -16,9 +17,9 @@
     return jnp.dot(a, b, preferred_element_type=f32)
 
 
-def moe_kernel(num_ep, local, cap, top_k, ids_ref, slot_ref, gval_ref, tok_ref, gate_ref, sw1, sw3, sw2, ew1, ew3, ew2, out_ref,
-               tb, mb, r_mine, r_out, r_in, w1s, w3s, w2s, s1, sd, got1, gotd, got2, h_ref, xs, gma, gmb,
-               w_sem, t_send, t_recv, m_send, m_recv, r_send, r_recv, s_send, s_recv):
+def moe_kernel(num_ep, local, cap, top_k, ids_hbm, slot_hbm, gval_hbm, tok_hbm, gate_ref, sw1, sw3, sw2, ew1, ew3, ew2, out_hbm,
+               out_ref, tok_ref, ids_ref, slot_ref, gval_ref, tb, mb, r_mine, r_out, r_in, w1s, w3s, w2s, s1, sd, got1, gotd, got2, h_ref, xs, gma, gmb,
+               i_sem, o_sem, w_sem, t_send, t_recv, m_send, m_recv, r_send, r_recv, s_send, s_recv):
     tok_count, hidden = tok_ref.shape
     ff = w1s.shape[2]
     rows = local * cap
@@ -52,6 +53,15 @@
         for c in weight_copies(ew1.at[0], ew3.at[0], ew2.at[0], slot):
             c.wait()
 
+    barrier = pltpu.get_barrier_semaphore()
+    for dev in (n1, n2, part):
+        pl.semaphore_signal(barrier, inc=1, device_id={'ep': dev}, device_id_type=pl.DeviceIdType.MESH)
+    loads = [pltpu.make_async_copy(src, dst, i_sem.at[k]) for k, (src, dst) in enumerate((
+        (ids_hbm, ids_ref), (slot_hbm, slot_ref), (gval_hbm, gval_ref), (tok_hbm, tok_ref)))]
+    for c in loads:
+        c.start()
+    for c in loads:
+        c.wait()
     for e in range(SLOTS):
         start_expert(e, e)
 
@@ -61,10 +71,7 @@
     mb[7, 8:8 + top_k, :] = jnp.where(kept, 0.5 * gval_ref[...], 0.0)
     mb[7, 8 + top_k:16, :] = jnp.zeros((8 - top_k, tok_count), f32)
 
-    barrier = pltpu.get_barrier_semaphore()
-    for k in range(1, num_ep):
-        pl.semaphore_signal(barrier, inc=1, device_id={'ep': (me + k) % num_ep}, device_id_type=pl.DeviceIdType.MESH)
-    pl.semaphore_wait(barrier, num_ep - 1)
+    pl.semaphore_wait(barrier, 3)
 
     class Hop:
         def __init__(self, src, dst, dev):
@@ -85,6 +92,9 @@
 
     t_own, t_n1, t_n1p, t_d, t_dp, t_n2, t_n2p = (
         Hop(7, 0, part), Hop(7, 1, n1), Hop(1, 2, part), Hop(1, 3, n2), Hop(3, 4, part), Hop(7, 5, n2), Hop(5, 6, part))
+    head, tail = pl.ds(0, HEAD), pl.ds(HEAD, tok_count - HEAD)
+    t_head = remote(tok_ref.at[head], tb.at[5, head], t_send.at[7], t_recv.at[7], n2)
+    t_n2.copies = (t_n2.copies[0], remote(tok_ref.at[tail], tb.at[5, tail], t_send.at[5], t_recv.at[5], n2))
     t_n1.start()
     t_own.start()
 
@@ -106,7 +116,7 @@
     def whole_rows(par):
         return remote(r_out, r_in.at[par], r_send, r_recv.at[par], part)
 
-    def expert_loop(order, par, keep, mine, other, mi, oi, late=None):
+    def expert_loop(order, par, keep, mine, other, mi, oi, late=()):
         def dispatch(e):
             base = ((me * local + e) * cap).astype(f32)
             for u, (unit, who) in enumerate(((mine, mi), (other, oi))):
@@ -122,8 +132,8 @@
         dispatch(jnp.int32(0))
 
         def body(e, _):
-            if late is not None:
-                pl.when(e == local - 1)(late)
+            for at, what in late:
+                pl.when(e == at)(what)
             slot = (order * local + e) % SLOTS
             wait_weights(slot)
 
@@ -223,7 +233,7 @@
         t_n2.start()
 
     t_own.wait_recv()
-    expert_loop(0, 2, 1, tok_ref, tb.at[0], 7, 0, late=first_tokens)
+    expert_loop(0, 2, 1, tok_ref, tb.at[0], 7, 0, late=((local - 3, t_head.start), (local - 1, first_tokens)))
     t_n1p.wait_recv()
     whole_rows(2).wait_send()
 
@@ -234,6 +244,7 @@
     t_dp.wait_recv()
 
     expert_loop(2, 1, 0, tb.at[3], tb.at[4], 3, 4)
+    t_head.wait_recv()
     t_n2.wait_recv()
     t_n2p.start()
     combine(1, 0, 3, nothing, put_sd, lambda i, rs: s_copy(1, i, rs).start(), lambda: whole_rows(1).wait())
@@ -276,9 +287,12 @@
         s_copy(0, c, rs).wait_recv()
         s_copy(2, c, rs).wait_recv()
         out_ref[rs, :] = (sd[rs, :] + got1[rs, :] + got2[rs, :]).astype(bf16)
+        pltpu.make_async_copy(out_ref.at[rs], out_hbm.at[rs], o_sem.at[c]).start()
     for c in range(chunks):
-        s_copy(2, c, chunk_rows(c)).wait_send()
-    for t in (t_own, t_n1, t_n1p, t_d, t_dp, t_n2, t_n2p):
+        rs = chunk_rows(c)
+        s_copy(2, c, rs).wait_send()
+        pltpu.make_async_copy(out_ref.at[rs], out_hbm.at[rs], o_sem.at[c]).wait()
+    for t in (t_head, t_own, t_n1, t_n1p, t_d, t_dp, t_n2, t_n2p):
         t.wait_send()
 
 
@@ -302,9 +316,14 @@
         return pl.pallas_call(
             functools.partial(moe_kernel, num_ep, local, cap, top_k),
             out_shape=jax.ShapeDtypeStruct((tok_count, hidden), bf16),
-            in_specs=[vm] * 5 + [hbm] * 6,
-            out_specs=vm,
+            in_specs=[hbm] * 4 + [vm] + [hbm] * 6,
+            out_specs=hbm,
             scratch_shapes=[
+                pltpu.VMEM((tok_count, hidden), bf16),
+                pltpu.VMEM((tok_count, hidden), bf16),
+                pltpu.VMEM((top_k, tok_count), jnp.int32),
+                pltpu.VMEM((top_k, tok_count), jnp.int32),
+                pltpu.VMEM((top_k, tok_count), f32),
                 pltpu.VMEM((7, tok_count, hidden), bf16),
                 pltpu.VMEM((8, 16, tok_count), f32),
                 pltpu.VMEM((2, rows, hidden), bf16),
@@ -318,7 +337,7 @@
                 pltpu.VMEM((2 * cap, hidden), bf16),
                 pltpu.VMEM((3, CHUNK, 2 * rows), bf16),
                 pltpu.VMEM((3, CHUNK, 2 * rows), bf16),
-                dma((SLOTS, 3)), dma((7,)), dma((7,)), dma((7,)), dma((7,)),
+                dma((4,)), dma((chunks,)), dma((SLOTS, 3)), dma((8,)), dma((8,)), dma((7,)), dma((7,)),
                 dma, dma((3,)), dma((3, chunks)), dma((3, chunks)),
             ],
             compiler_params=pltpu.CompilerParams(collective_id=0, has_side_effects=True, vmem_limit_bytes=67043328),

time: 143 us -> 138 us (0.965)
  Pallas kernels: 140 us -> 135 us
    pallas_call x1, Pallas kernels: 140 us -> 135 us  [device_step(): pl.pallas_call(functools.partial(moe_kernel, num_ep, local, cap, top_k),...]
where the time goes in v3:
time: 138 us
  Pallas kernels  135 us (98%)
  local copies, waits for them, and re-layouts  2.46 us (2%)
    pallas_call x1, Pallas kernels, device_step(): pl.pallas_call(functools.partial(moe_kernel, num_ep, local, cap, top_k),...  135 us

profile of v3, /device:TPU:0, one launch (start us, length us, event | category | flops | bytes accessed | tf_op | source)
XLA Modules:
  0.0 137.6 jit_solution(16657275739699074313)
XLA Ops:
  0.0 135.1 %shard_map.109 = bf16[512,1280]{1,0:T(8,128)(2,1)} custom-call(s32[6,512]{1,0:T(8,128)} %bitcast.3, s32[6,512]{1,0:T(8,128)} %bitcast.4, f32[6,512]{1,0:T(8,128)} %bitcast.5, bf16[512,1280]{1,0:T(8,128)(2,1)} %tok_hbm.1, bf16[1280]{0:T(1024)(128)(2,1)} %gate_ref.1, bf16[1280,1792]{1,0:T(8,128)(2,1)} %sw1.1, bf16[1280,1792]{1,0:T(8,128)(2,1)} %sw3.1, ...), custom_call_target="tpu_custom_call" | custom-call | tf_op jit(solution)/shard_map/pallas_call | solution.py:316
  135.1 2.5 %copy.13 = bf16[512,1280]{1,0:T(8,128)(2,1)} copy(bf16[512,1280]{1,0:T(8,128)(2,1)} %shard_map.109) | data formatting | bytes 2621440

commit v4 on v3

--- a/solution.py
+++ b/solution.py
@@ -17,9 +17,9 @@
     return jnp.dot(a, b, preferred_element_type=f32)
 
 
-def moe_kernel(num_ep, local, cap, top_k, ids_hbm, slot_hbm, gval_hbm, tok_hbm, gate_ref, sw1, sw3, sw2, ew1, ew3, ew2, out_hbm,
-               out_ref, tok_ref, ids_ref, slot_ref, gval_ref, tb, mb, r_mine, r_out, r_in, w1s, w3s, w2s, s1, sd, got1, gotd, got2, h_ref, xs, gma, gmb,
-               i_sem, o_sem, w_sem, t_send, t_recv, m_send, m_recv, r_send, r_recv, s_send, s_recv):
+def moe_kernel(num_ep, local, cap, top_k, ids_hbm, slot_hbm, gval_hbm, tok_hbm, gate_ref, sw1, sw3, sw2, ew1, ew3, ew2, out_ref,
+               tok_ref, ids_ref, slot_ref, gval_ref, tb, mb, r_mine, r_out, r_in, w1s, w3s, w2s, s1, sd, got1, gotd, got2, h_ref, xs, gma, gmb,
+               i_sem, w_sem, t_send, t_recv, m_send, m_recv, r_send, r_recv, s_send, s_recv):
     tok_count, hidden = tok_ref.shape
     ff = w1s.shape[2]
     rows = local * cap
@@ -60,7 +60,34 @@
         (ids_hbm, ids_ref), (slot_hbm, slot_ref), (gval_hbm, gval_ref), (tok_hbm, tok_ref)))]
     for c in loads:
         c.start()
-    for c in loads:
+    loads[3].wait()
+    pl.semaphore_wait(barrier, 3)
+
+    class Hop:
+        def __init__(self, src, dst, dev):
+            self.copies = (remote(mb.at[src], mb.at[dst], m_send.at[dst], m_recv.at[dst], dev),
+                           remote(tok_ref if src == 7 else tb.at[src], tb.at[dst], t_send.at[dst], t_recv.at[dst], dev))
+
+        def start(self):
+            for c in self.copies:
+                c.start()
+
+        def wait_recv(self):
+            for c in self.copies:
+                c.wait_recv()
+
+        def wait_send(self):
+            for c in self.copies:
+                c.wait_send()
+
+    t_own, t_n1, t_n1p, t_d, t_dp, t_n2, t_n2p = (
+        Hop(7, 0, part), Hop(7, 1, n1), Hop(1, 2, part), Hop(1, 3, n2), Hop(3, 4, part), Hop(7, 5, n2), Hop(5, 6, part))
+    head, tail = pl.ds(0, HEAD), pl.ds(HEAD, tok_count - HEAD)
+    t_head = remote(tok_ref.at[head], tb.at[5, head], t_send.at[7], t_recv.at[7], n2)
+    t_n2.copies = (t_n2.copies[0], remote(tok_ref.at[tail], tb.at[5, tail], t_send.at[5], t_recv.at[5], n2))
+    t_n1.copies[1].start()
+    t_own.copies[1].start()
+    for c in loads[:3]:
         c.wait()
     for e in range(SLOTS):
         start_expert(e, e)
@@ -71,32 +98,8 @@
     mb[7, 8:8 + top_k, :] = jnp.where(kept, 0.5 * gval_ref[...], 0.0)
     mb[7, 8 + top_k:16, :] = jnp.zeros((8 - top_k, tok_count), f32)
 
-    pl.semaphore_wait(barrier, 3)
-
-    class Hop:
-        def __init__(self, src, dst, dev):
-            self.copies = (remote(mb.at[src], mb.at[dst], m_send.at[dst], m_recv.at[dst], dev),
-                           remote(tok_ref if src == 7 else tb.at[src], tb.at[dst], t_send.at[dst], t_recv.at[dst], dev))
-
-        def start(self):
-            for c in self.copies:
-                c.start()
-
-        def wait_recv(self):
-            for c in self.copies:
-                c.wait_recv()
-
-        def wait_send(self):
-            for c in self.copies:
-                c.wait_send()
-
-    t_own, t_n1, t_n1p, t_d, t_dp, t_n2, t_n2p = (
-        Hop(7, 0, part), Hop(7, 1, n1), Hop(1, 2, part), Hop(1, 3, n2), Hop(3, 4, part), Hop(7, 5, n2), Hop(5, 6, part))
-    head, tail = pl.ds(0, HEAD), pl.ds(HEAD, tok_count - HEAD)
-    t_head = remote(tok_ref.at[head], tb.at[5, head], t_send.at[7], t_recv.at[7], n2)
-    t_n2.copies = (t_n2.copies[0], remote(tok_ref.at[tail], tb.at[5, tail], t_send.at[5], t_recv.at[5], n2))
-    t_n1.start()
-    t_own.start()
+    t_n1.copies[0].start()
+    t_own.copies[0].start()
 
     def swiglu_up(x, slot, put):
         full = ff // 256
@@ -287,11 +290,9 @@
         s_copy(0, c, rs).wait_recv()
         s_copy(2, c, rs).wait_recv()
         out_ref[rs, :] = (sd[rs, :] + got1[rs, :] + got2[rs, :]).astype(bf16)
-        pltpu.make_async_copy(out_ref.at[rs], out_hbm.at[rs], o_sem.at[c]).start()
     for c in range(chunks):
         rs = chunk_rows(c)
         s_copy(2, c, rs).wait_send()
-        pltpu.make_async_copy(out_ref.at[rs], out_hbm.at[rs], o_sem.at[c]).wait()
     for t in (t_head, t_own, t_n1, t_n1p, t_d, t_dp, t_n2, t_n2p):
         t.wait_send()
 
@@ -315,11 +316,10 @@
         dma = pltpu.SemaphoreType.DMA
         return pl.pallas_call(
             functools.partial(moe_kernel, num_ep, local, cap, top_k),
-            out_shape=jax.ShapeDtypeStruct((tok_count, hidden), bf16),
+            out_shape=pltpu.VMEM((tok_count, hidden), bf16),
             in_specs=[hbm] * 4 + [vm] + [hbm] * 6,
-            out_specs=hbm,
+            out_specs=vm,
             scratch_shapes=[
-                pltpu.VMEM((tok_count, hidden), bf16),
                 pltpu.VMEM((tok_count, hidden), bf16),
                 pltpu.VMEM((top_k, tok_count), jnp.int32),
                 pltpu.VMEM((top_k, tok_count), jnp.int32),
@@ -337,10 +337,10 @@
                 pltpu.VMEM((2 * cap, hidden), bf16),
                 pltpu.VMEM((3, CHUNK, 2 * rows), bf16),
                 pltpu.VMEM((3, CHUNK, 2 * rows), bf16),
-                dma((4,)), dma((chunks,)), dma((SLOTS, 3)), dma((8,)), dma((8,)), dma((7,)), dma((7,)),
+                dma((4,)), dma((SLOTS, 3)), dma((8,)), dma((8,)), dma((7,)), dma((7,)),
                 dma, dma((3,)), dma((3, chunks)), dma((3, chunks)),
             ],
-            compiler_params=pltpu.CompilerParams(collective_id=0, has_side_effects=True, vmem_limit_bytes=67043328),
+            compiler_params=pltpu.CompilerParams(collective_id=0, has_side_effects=True, vmem_limit_bytes=64000000),
         )(expert_ids.T, slots.T, gate_vals.T, tokens, shared_gate, shared_w1, shared_w3, shared_w2, expert_w1, expert_w3, expert_w2)
 
     return jax.shard_map(device_step, mesh=mesh, in_specs=(row_spec, row_spec, row_spec, row_spec, replicated, replicated, replicated, replicated, expert_spec, expert_spec, expert_spec), out_specs=row_spec, check_vma=False)

time: 138 us -> 136 us (0.986)
  local copies, waits for them, and re-layouts: 2.46 us -> 1.06 us
    unnamed x1, local copies, waits for them, and re-layouts: 2.46 us -> 1.06 us
where the time goes in v4:
time: 136 us; the launch traced here: 135 us
  Pallas kernels  134 us (99%)
    pallas_call x1, Pallas kernels, device_step(): pl.pallas_call(functools.partial(moe_kernel, num_ep, local, cap, top_k),...  134 us

profile of v4, /device:TPU:0, one launch (start us, length us, event | category | flops | bytes accessed | tf_op | source)
XLA Modules:
  0.0 135.4 jit_solution(13464732904733268122)
XLA Ops:
  0.0 134.3 %shard_map.109 = bf16[512,1280]{1,0:T(8,128)(2,1)S(1)} custom-call(s32[6,512]{1,0:T(8,128)} %bitcast.3, s32[6,512]{1,0:T(8,128)} %bitcast.4, f32[6,512]{1,0:T(8,128)} %bitcast.5, bf16[512,1280]{1,0:T(8,128)(2,1)} %tok_hbm.1, bf16[1280]{0:T(1024)(128)(2,1)} %gate_ref.1, bf16[1280,1792]{1,0:T(8,128)(2,1)} %sw1.1, bf16[1280,1792]{1,0:T(8,128)(2,1)} %sw3.1, ...), custom_call_target="tpu_custom_call" | custom-call | tf_op jit(solution)/shard_map/pallas_call | solution.py:317
  134.3 1.1 copy.13

commit v5 on v4

--- a/solution.py
+++ b/solution.py
@@ -17,8 +17,8 @@
     return jnp.dot(a, b, preferred_element_type=f32)
 
 
-def moe_kernel(num_ep, local, cap, top_k, ids_hbm, slot_hbm, gval_hbm, tok_hbm, gate_ref, sw1, sw3, sw2, ew1, ew3, ew2, out_ref,
-               tok_ref, ids_ref, slot_ref, gval_ref, tb, mb, r_mine, r_out, r_in, w1s, w3s, w2s, s1, sd, got1, gotd, got2, h_ref, xs, gma, gmb,
+def moe_kernel(num_ep, local, cap, top_k, ids_hbm, slot_hbm, gval_hbm, tok_hbm, gate_hbm, sw1, sw3, sw2, ew1, ew3, ew2, out_ref,
+               tok_ref, ids_ref, slot_ref, gval_ref, gate_ref, tb, mb, r_mine, r_out, r_in, w1s, w3s, w2s, s1, sd, got1, gotd, got2, h_ref, xs, gma, gmb,
                i_sem, w_sem, t_send, t_recv, m_send, m_recv, r_send, r_recv, s_send, s_recv):
     tok_count, hidden = tok_ref.shape
     ff = w1s.shape[2]
@@ -57,7 +57,7 @@
     for dev in (n1, n2, part):
         pl.semaphore_signal(barrier, inc=1, device_id={'ep': dev}, device_id_type=pl.DeviceIdType.MESH)
     loads = [pltpu.make_async_copy(src, dst, i_sem.at[k]) for k, (src, dst) in enumerate((
-        (ids_hbm, ids_ref), (slot_hbm, slot_ref), (gval_hbm, gval_ref), (tok_hbm, tok_ref)))]
+        (ids_hbm, ids_ref), (slot_hbm, slot_ref), (gval_hbm, gval_ref), (tok_hbm, tok_ref), (gate_hbm, gate_ref)))]
     for c in loads:
         c.start()
     loads[3].wait()
@@ -87,7 +87,7 @@
     t_n2.copies = (t_n2.copies[0], remote(tok_ref.at[tail], tb.at[5, tail], t_send.at[5], t_recv.at[5], n2))
     t_n1.copies[1].start()
     t_own.copies[1].start()
-    for c in loads[:3]:
+    for c in loads[:3] + loads[4:]:
         c.wait()
     for e in range(SLOTS):
         start_expert(e, e)
@@ -317,13 +317,14 @@
         return pl.pallas_call(
             functools.partial(moe_kernel, num_ep, local, cap, top_k),
             out_shape=pltpu.VMEM((tok_count, hidden), bf16),
-            in_specs=[hbm] * 4 + [vm] + [hbm] * 6,
+            in_specs=[hbm] * 11,
             out_specs=vm,
             scratch_shapes=[
                 pltpu.VMEM((tok_count, hidden), bf16),
                 pltpu.VMEM((top_k, tok_count), jnp.int32),
                 pltpu.VMEM((top_k, tok_count), jnp.int32),
                 pltpu.VMEM((top_k, tok_count), f32),
+                pltpu.VMEM((hidden,), bf16),
                 pltpu.VMEM((7, tok_count, hidden), bf16),
                 pltpu.VMEM((8, 16, tok_count), f32),
                 pltpu.VMEM((2, rows, hidden), bf16),
@@ -337,7 +338,7 @@
                 pltpu.VMEM((2 * cap, hidden), bf16),
                 pltpu.VMEM((3, CHUNK, 2 * rows), bf16),
                 pltpu.VMEM((3, CHUNK, 2 * rows), bf16),
-                dma((4,)), dma((SLOTS, 3)), dma((8,)), dma((8,)), dma((7,)), dma((7,)),
+                dma((5,)), dma((SLOTS, 3)), dma((8,)), dma((8,)), dma((7,)), dma((7,)),
                 dma, dma((3,)), dma((3, chunks)), dma((3, chunks)),
             ],
             compiler_params=pltpu.CompilerParams(collective_id=0, has_side_effects=True, vmem_limit_bytes=64000000),

time: 136 us -> 135 us (level)
  no operation moved by 1% of the time
where the time goes in v5:
time: 135 us
  Pallas kernels  134 us (99%)
    pallas_call x1, Pallas kernels, device_step(): pl.pallas_call(functools.partial(moe_kernel, num_ep, local, cap, top_k),...  134 us

profile of v5, /device:TPU:0, one launch (start us, length us, event | category | flops | bytes accessed | tf_op | source)
XLA Modules:
  0.0 134.7 jit_solution(17511006182073275181)
XLA Ops:
  0.0 133.6 %shard_map.109 = bf16[512,1280]{1,0:T(8,128)(2,1)S(1)} custom-call(s32[6,512]{1,0:T(8,128)} %bitcast.3, s32[6,512]{1,0:T(8,128)} %bitcast.4, f32[6,512]{1,0:T(8,128)} %bitcast.5, bf16[512,1280]{1,0:T(8,128)(2,1)} %tok_hbm.1, bf16[1280]{0:T(1024)(128)(2,1)} %gate_hbm.1, bf16[1280,1792]{1,0:T(8,128)(2,1)} %sw1.1, bf16[1280,1792]{1,0:T(8,128)(2,1)} %sw3.1, ...), custom_call_target="tpu_custom_call" | custom-call | tf_op jit(solution)/shard_map/pallas_call | solution.py:317
  133.6 1.1 copy.13

commit v6 on v5

--- a/solution.py
+++ b/solution.py
@@ -94,9 +94,7 @@
 
     kept = slot_ref[...] >= 0
     mb[7, 0:top_k, :] = jnp.where(kept, ids_ref[...] * cap + slot_ref[...], -1).astype(f32)
-    mb[7, top_k:8, :] = jnp.full((8 - top_k, tok_count), -1.0, f32)
-    mb[7, 8:8 + top_k, :] = jnp.where(kept, 0.5 * gval_ref[...], 0.0)
-    mb[7, 8 + top_k:16, :] = jnp.zeros((8 - top_k, tok_count), f32)
+    mb[7, top_k:2 * top_k, :] = jnp.where(kept, 0.5 * gval_ref[...], 0.0)
 
     t_n1.copies[0].start()
     t_own.copies[0].start()
@@ -123,7 +121,7 @@
         def dispatch(e):
             base = ((me * local + e) * cap).astype(f32)
             for u, (unit, who) in enumerate(((mine, mi), (other, oi))):
-                d = mb[who, 0:8, :] - base
+                d = mb[who, 0:top_k, :] - base
                 hit = d[0:1, :] == lane_row
                 for k in range(1, top_k):
                     hit = hit | (d[k:k + 1, :] == lane_row)
@@ -174,9 +172,9 @@
                 base = (owner * rows).astype(f32)
                 for c in range(nr):
                     rid = lane_col + (base + c * 128.0)
-                    g = jnp.where(m[:, 0:1] == rid, m[:, 8:9], 0.0)
+                    g = jnp.where(m[:, 0:1] == rid, m[:, top_k:top_k + 1], 0.0)
                     for k in range(1, top_k):
-                        g = jnp.where(m[:, k:k + 1] == rid, m[:, 8 + k:9 + k], g)
+                        g = jnp.where(m[:, k:k + 1] == rid, m[:, top_k + k:top_k + k + 1], g)
                     g1 = g.astype(bf16)
                     rem = g - g1.astype(f32)
                     g2 = rem.astype(bf16)
@@ -264,6 +262,8 @@
     combine(2, 1, 7, nothing, put_sd, nothing, lambda: whole_rows(2).wait_recv())
 
     mrows = 256
+    for c in range(chunks):
+        s_copy(0, c, chunk_rows(c)).wait_recv()
     for s in range(2):
         slot = (4 * local + s) % SLOTS
         wait_weights(slot)
@@ -280,16 +280,15 @@
                 cols = slice(n * 256, n * 256 + 256)
                 v = sd[rs, cols] + sig * dot(h_ref[...], w2s[slot, :, cols])
                 if s == 1:
-                    v = v + tok_ref[rs, cols].astype(f32)
+                    v = v + tok_ref[rs, cols].astype(f32) + got1[rs, cols]
                 sd[rs, cols] = v
             return 0
         lax.fori_loop(0, tok_count // mrows, block, 0)
 
     for c in range(chunks):
         rs = chunk_rows(c)
-        s_copy(0, c, rs).wait_recv()
         s_copy(2, c, rs).wait_recv()
-        out_ref[rs, :] = (sd[rs, :] + got1[rs, :] + got2[rs, :]).astype(bf16)
+        out_ref[rs, :] = (sd[rs, :] + got2[rs, :]).astype(bf16)
     for c in range(chunks):
         rs = chunk_rows(c)
         s_copy(2, c, rs).wait_send()
@@ -326,7 +325,7 @@
                 pltpu.VMEM((top_k, tok_count), f32),
                 pltpu.VMEM((hidden,), bf16),
                 pltpu.VMEM((7, tok_count, hidden), bf16),
-                pltpu.VMEM((8, 16, tok_count), f32),
+                pltpu.VMEM((8, 2 * top_k, tok_count), f32),
                 pltpu.VMEM((2, rows, hidden), bf16),
                 pltpu.VMEM((rows, hidden), bf16),
                 pltpu.VMEM((3, rows, hidden), bf16),

time: 135 us -> 135 us (level)
  no operation moved by 1% of the time
where the time goes in v6:
time: 135 us
  Pallas kernels  134 us (99%)
    pallas_call x1, Pallas kernels, device_step(): pl.pallas_call(functools.partial(moe_kernel, num_ep, local, cap, top_k),...  134 us

profile of v6, /device:TPU:0, one launch (start us, length us, event | category | flops | bytes accessed | tf_op | source)
XLA Modules:
  0.0 134.7 jit_solution(2775809453391287054)
XLA Ops:
  0.0 133.6 %shard_map.109 = bf16[512,1280]{1,0:T(8,128)(2,1)S(1)} custom-call(s32[6,512]{1,0:T(8,128)} %bitcast.3, s32[6,512]{1,0:T(8,128)} %bitcast.4, f32[6,512]{1,0:T(8,128)} %bitcast.5, bf16[512,1280]{1,0:T(8,128)(2,1)} %tok_hbm.1, bf16[1280]{0:T(1024)(128)(2,1)} %gate_hbm.1, bf16[1280,1792]{1,0:T(8,128)(2,1)} %sw1.1, bf16[1280,1792]{1,0:T(8,128)(2,1)} %sw3.1, ...), custom_call_target="tpu_custom_call" | custom-call | tf_op jit(solution)/shard_map/pallas_call | solution.py:316
  133.6 1.1 copy.13
